TPU v7x, 32 devices: a whole 2x2x4 slice. The times are simulated.
32 devices in a mesh: band: 4 (over z), sector: 8 (over y, x, core).
Axes of the slice: x: 2, y: 2, z: 4, core: 2. Of those that a mesh axis runs over, the one named last changes fastest.
Arguments:
- field: float32 [2, 640, 2, 2560], P(None, 'band', None, 'sector'), may hold values from -6 to 6
- depart: int32 [2, 640, 80], P(None, 'band', 'sector'), may hold values from -2 to 2
- interp_weight: bfloat16 [2, 640, 80, 64, 32], P(None, 'band', 'sector'), may hold values from -0.75 to 0.75
- legendre: float32 [640, 640, 1281], P('sector', 'band'), may hold values from -0.25 to 0.25
- damping: float32 [2], replicated, may hold values from 0.3 to 30
Outputs:
- new_field: float32 [2, 640, 2, 2560], P(None, 'band', None, 'sector')
All inputs are finite; a program needn't handle non-finite values.
Results may differ from a plain program's by a relative error of at most 0.0003.
Values sent between devices are 32-bit elements; how exact they have to be, the bound alone decides.
No kernel may reach another device: no remote copies, remote signals or barrier semaphores. Data moves between devices by JAX's collectives and lax.ppermute only.
A program may use at most 192 MiB of HBM per device.

v0:
```python
import math
import jax
import jax.numpy as jnp
from jax import lax
from jax.sharding import PartitionSpec as P

HIGHEST = lax.Precision.HIGHEST


def padded(x, sides, width):
    for axis, dim in sides:
        peers, length = (lax.axis_size(axis), x.shape[dim])
        up = [(i, (i + 1) % peers) for i in range(peers)]
        down = [(j, i) for i, j in up]
        last = lax.slice_in_dim(x, length - width, length, axis=dim)
        leading = lax.slice_in_dim(x, 0, width, axis=dim)
        before = lax.ppermute(last, axis, up)
        after = lax.ppermute(leading, axis, down)
        x = jnp.concatenate([before, x, after], axis=dim)
    return x


def phase(product, lon_count):
    return 2.0 * math.pi / lon_count * (product % lon_count).astype(jnp.float32)


def forward_table(lon_count, m_count, pair_total):
    longitude = jnp.arange(lon_count, dtype=jnp.int32)[:, None]
    pair_range = jnp.arange(pair_total, dtype=jnp.int32)[None, :]
    lower_angle = phase(longitude * pair_range, lon_count)
    upper_angle = phase(longitude * (m_count - 1 - pair_range), lon_count)
    table = jnp.stack(
        [jnp.cos(lower_angle), -jnp.sin(lower_angle), jnp.cos(upper_angle), -jnp.sin(upper_angle)],
        axis=1,
    )
    return table / lon_count


def inverse_table(lon_count, m_count, pair_total):
    pair_range = jnp.arange(pair_total, dtype=jnp.int32)[:, None]
    longitude = jnp.arange(lon_count, dtype=jnp.int32)[None, :]
    lower_angle = phase(pair_range * longitude, lon_count)
    upper_angle = phase((m_count - 1 - pair_range) * longitude, lon_count)
    lower_scale = jnp.where(pair_range == 0, 1.0, 2.0)
    return jnp.stack(
        [
            lower_scale * jnp.cos(lower_angle),
            -lower_scale * jnp.sin(lower_angle),
            2.0 * jnp.cos(upper_angle),
            -2.0 * jnp.sin(upper_angle),
        ],
        axis=0,
    )


def pair_masks(pair_index, m_count, row_count):
    column = jnp.arange(row_count, dtype=jnp.int32)[None, :]
    limit = (m_count - pair_index)[:, None]
    leading = column < limit
    lag_value = jnp.where(leading, column, column - limit)
    odd_rows = lag_value % 2 == 1
    degree = jnp.where(leading, pair_index[:, None] + column, column - 1)
    return (leading, odd_rows, degree)


def analyse(wave, legendre, leading, odd_rows):
    stacked = jnp.stack([wave[0] + wave[1], wave[0] - wave[1]])
    product = jnp.einsum("svcpl,plk->svcpk", stacked, legendre, precision=HIGHEST)
    chosen = jnp.where(odd_rows, product[1], product[0])
    return jnp.where(leading, chosen[:, 0:2], chosen[:, 2:4])


def solve_modes(spectrum, damping_levels, degree, m_count):
    ratio = (degree * (degree + 1)).astype(jnp.float32) / float(m_count * m_count)
    return spectrum / (1.0 + damping_levels[:, None, None, None] * ratio[None, None])


def synthesise(spectrum, legendre, leading, odd_rows):
    lower = jnp.where(leading, spectrum, 0.0)
    upper = jnp.where(leading, 0.0, spectrum)
    northern = jnp.concatenate([lower, upper], axis=1)
    southern = jnp.where(odd_rows, -northern, northern)
    stacked = jnp.stack([northern, southern])
    return jnp.einsum("hvcpk,plk->hvcpl", stacked, legendre, precision=HIGHEST)


def advect(field, depart, interp_weight):
    tile_width = interp_weight.shape[-1]
    tile_count = depart.shape[2]
    extended = padded(field, (("sector", 3),), 3 * tile_width)
    pieces = extended.reshape(
        field.shape[0], field.shape[1], field.shape[2], tile_count + 6, tile_width
    )
    window = jnp.zeros(field.shape[:3] + (tile_count, 2 * tile_width), jnp.float32)
    for offset in range(-2, 3):
        lead_part = pieces[:, :, :, 3 + offset : 3 + offset + tile_count]
        next_part = pieces[:, :, :, 4 + offset : 4 + offset + tile_count]
        candidate = jnp.concatenate([lead_part, next_part], axis=4)
        window = jnp.where((depart == offset)[:, :, None, :, None], candidate, window)
    result = jnp.einsum(
        "hlvtj,hltji->hlvti", window, interp_weight.astype(jnp.float32), precision=HIGHEST
    )
    return result.reshape(field.shape)


def local(field, depart, interp_weight, legendre, damping):
    advected = advect(field, depart, interp_weight)
    columns = lax.all_to_all(advected, "sector", split_axis=1, concat_axis=3, tiled=True)
    lon_count = columns.shape[3]
    row_count = legendre.shape[2]
    m_count = row_count - 1
    pair_total = m_count // 2
    fourier = jnp.einsum(
        "hlvn,ncp->hvcpl", columns, forward_table(lon_count, m_count, pair_total), precision=HIGHEST
    )
    wave = lax.all_to_all(fourier, "sector", split_axis=3, concat_axis=4, tiled=True)
    pair_local = legendre.shape[0]
    pair_index = lax.axis_index("sector") * pair_local + jnp.arange(pair_local, dtype=jnp.int32)
    leading, odd_rows, degree = pair_masks(pair_index, m_count, row_count)
    partial_value = analyse(wave, legendre, leading, odd_rows)
    summed = lax.psum(partial_value, "band")
    spectrum = solve_modes(summed, damping, degree, m_count)
    synthesis = synthesise(spectrum, legendre, leading, odd_rows)
    returned = lax.all_to_all(synthesis, "sector", split_axis=4, concat_axis=3, tiled=True)
    gridded = jnp.einsum(
        "hvcpl,cpn->hlvn",
        returned,
        inverse_table(lon_count, m_count, pair_total),
        precision=HIGHEST,
    )
    return lax.all_to_all(gridded, "sector", split_axis=3, concat_axis=1, tiled=True)


def solution(mesh):
    return jax.shard_map(
        local,
        mesh=mesh,
        in_specs=(
            P(None, "band", None, "sector"),
            P(None, "band", "sector"),
            P(None, "band", "sector", None, None),
            P("sector", "band", None),
            P(),
        ),
        out_specs=P(None, "band", None, "sector"),
        check_vma=False,
    )
```

profile of v0, /device:TPU:0, one launch (start us, length us, event | category | flops | bytes accessed | tf_op | source)
XLA Modules:
  0.0 574.6 jit_solution(14221418994076441532)
XLA Ops:
  6.5 1.6 copy.106
  8.1 0.1 fusion.71
  8.2 0.5 collective-permute-start
  8.7 2.9 collective-permute-start.1
  11.6 28.4 %fusion.32 = (f32[2560,1,640]{2,0,1:T(8,128)}, f32[2560,1,640]{2,0,1:T(8,128)}) fusion(s32[640]{0:T(1024)S(1)} %iota_subtract_fusion), kind=kLoop, calls=%fused_computation.40 | loop fusion | flops 16384000 | bytes 13109760 | tf_op jit(solution)/shard_map/cos | solution.py:33
  40.0 0.1 broadcast_compare_fusion.4
  40.2 47.9 %copy.114 = bf16[2,160,10,64,32]{3,4,2,1,0:T(8,128)(2,1)} copy(bf16[2,160,10,64,32]{1,4,3,2,0:T(8,128)(2,1)} %param.7) | data formatting | bytes 26214400 | tf_op args[2]
  88.1 0.1 pad_maximum_fusion.1
  88.2 1.0 fusion.70
  89.3 1.8 maximum_select_fusion
  91.1 3.6 copy.113
  94.7 43.8 %convolution_bitcast_fusion = f32[2,160,2,10,32]{4,2,3,1,0:T(2,128)S(1)} fusion(f32[2,160,2,10,64]{4,2,3,1,0:T(2,128)} %copy.113, bf16[2,160,10,64,32]{3,4,2,1,0:T(8,128)(2,1)} %copy.114), kind=kOutput, calls=%fused_computation.67 | convolution fusion | flops 157286400 | bytes 15564800 | tf_op jit(solution)/shard_map/hlvtj,hltji->hlvti/dot_general | solution.py:100
  138.4 3.4 copy.115
  141.8 2.4 copy.116
  144.2 4.0 all-to-all-start
  148.2 27.9 %sine_negate_fusion.1 = (f32[2560,1,640]{2,0,1:T(8,128)}, f32[2560,1,640]{2,0,1:T(8,128)}) fusion(), kind=kLoop, calls=%fused_computation.41 | loop fusion | flops 16384000 | bytes 13107200 | tf_op jit(solution)/shard_map/neg | solution.py:33
  176.1 0.0 all-to-all-done
  176.1 0.3 copy.140
  176.4 0.3 reshape.528
  176.7 19.3 %fusion.54 = f32[2,2,4,640,20]{3,4,1,0,2:T(8,128)S(1)} fusion(f32[2,20,2,2560,1]{3,1,2,0,4:T(8,128)S(1)} %reshape.528, f32[2560,1,640]{2,0,1:T(8,128)} %get-tuple-element.25, f32[2560,1,640]{2,0,1:T(8,128)} %get-tuple-element.24, f32[2560,1,640]{2,0,1:T(8,128)} %get-tuple-element.30, f32[2560,1,640]{2,0,1:T(8,128)} %get-tuple-element.31), kind=kOutput, calls=%fused_computation.78 | convolution fusion | flops 6317670400 | bytes 27852800 | tf_op jit(solution)/shard_map/hlvn,ncp->hvcpl/dot_general | solution.py:113
  196.0 5.0 copy.120
  201.0 10.6 %reshape.535 = f32[8,1,25600]{2,1,0:T(1,128)} reshape(f32[640,4,2,2,20]{4,3,2,1,0:T(2,128)} %bitcast.90) | data formatting | bytes 1638400
  211.6 4.2 all-to-all-start.1
  215.8 0.0 all-reduce.2.cloned.1.call-start
  215.8 1.0 fusion.61
  216.9 0.2 fusion.63
  217.1 11.6 %all-to-all-done.1 = f32[8,1,25600]{2,1,0:T(1,128)S(1)} async-done(((f32[8,1,25600]{2,1,0:T(1,128)}), f32[8,1,25600]{2,1,0:T(1,128)S(1)}, u32[]{:S(2)}, u32[]{:S(2)}) %all-to-all-start.1) | async-done | bytes 819232 | tf_op jit(solution)/shard_map/all_to_all | solution.py:116
  228.7 0.5 broadcast.505
  229.2 2.6 reduce
  231.8 10.9 %reshape.536 = f32[640,4,2,2,20]{4,3,2,1,0:T(2,128)} reshape(f32[8,25600]{1,0:T(8,128)S(1)} %reduce) | data formatting | bytes 1638400
  242.7 6.0 %copy.141 = f32[2,2,4,8,80,20]{4,3,2,5,1,0:T(8,128)S(1)} copy(f32[2,2,4,8,80,20]{5,1,0,2,4,3:T(2,128)} %bitcast.91) | data formatting | bytes 1638400 | tf_op jit(solution)/shard_map/all_to_all | solution.py:116
  248.7 0.2 slice_add_fusion
  248.8 0.2 copy.122
  249.0 0.4 copy.124
  249.4 0.2 copy.123
  249.6 0.4 copy.125
  250.1 0.3 fusion.83
  250.4 42.7 %fusion.44 = f32[2,2,4,80,1281]{4,2,1,0,3:T(4,128)} fusion(f32[80,160,1281]{2,1,0:T(8,128)} %param.8, f32[2,2,4,80,160]{4,2,1,0,3:T(4,128)S(1)} %fusion.83), kind=kOutput, calls=%fused_computation.61 | convolution fusion | flops 3148185600 | bytes 72965120 | tf_op jit(solution)/shard_map/svcpl,plk->svcpk/dot_general | solution.py:68
  293.2 4.5 fusion.48
  297.6 0.0 copy-start.2
  297.6 2.6 slice_select_fusion
  300.3 0.0 all-reduce.2.cloned.1.call-update
  300.3 0.5 multiply_add_fusion
  300.8 28.3 %sine_multiply_fusion.1 = (f32[1,640,2560]{2,1,0:T(8,128)}, f32[1,640,2560]{2,1,0:T(8,128)}) fusion(f32[640]{0:T(1024)S(1)} %fusion.65, f32[640]{0:T(1024)S(1)} %fusion.64), kind=kLoop, calls=%fused_computation.51 | loop fusion | flops 18022400 | bytes 13112320 | tf_op jit(solution)/shard_map/mul | solution.py:48
  329.0 48.0 %all-reduce.2.cloned.1.call-done = f32[2,2,80,1281]{3,1,0,2:T(2,128)} async-done(((f32[2,2,80,1281]{3,1,0,2:T(2,128)}), f32[2,2,80,1281]{3,1,0,2:T(2,128)}) %all-reduce.2.cloned.1.call-update) | async-done | bytes 1639696 | tf_op jit(solution)/shard_map/psum | solution.py:121
  377.0 3.1 broadcast_select_fusion.1
  380.1 1.1 broadcast_select_fusion
  381.3 1.1 fusion.76
  382.4 1.7 maximum_bitcast_fusion.4
  384.1 2.4 negate_select_fusion
  386.5 73.3 %fusion.49 = f32[2,2,4,80,160]{4,2,1,0,3:T(4,128)S(1)} fusion(f32[80,160,1281]{2,1,0:T(8,128)} %param.8, f32[1,2,4,80,1281]{4,2,1,3,0:T(4,128)S(1)} %negate_select_fusion, f32[1,2,4,80,1281]{4,2,1,3,0:T(4,128)S(1)} %maximum_bitcast_fusion.4), kind=kOutput, calls=%fused_computation.77 | convolution fusion | flops 3149825280 | bytes 72965120 | tf_op jit(solution)/shard_map/hvcpk,plk->hvcpl/dot_general | solution.py:84
  459.8 1.7 copy.128
  461.4 4.1 all-to-all-start.2
  465.6 29.7 %cosine_multiply_fusion = (f32[1,640,2560]{2,1,0:T(8,128)}, f32[1,640,2560]{2,1,0:T(8,128)}) fusion(s32[640]{0:T(1024)S(1)} %iota_subtract_fusion), kind=kLoop, calls=%fused_computation.47 | loop fusion | flops 18022400 | bytes 13109760 | tf_op jit(solution)/shard_map/mul | solution.py:49
  495.2 0.8 copy.143
  496.0 0.5 reshape.534
  496.5 19.2 %fusion.47 = f32[2,20,2,2560]{3,1,2,0:T(8,128)S(1)} fusion(f32[2,2,4,640,20]{3,4,2,1,0:T(8,128)S(1)} %reshape.534, f32[1,640,2560]{2,1,0:T(8,128)} %get-tuple-element.23, f32[1,640,2560]{2,1,0:T(8,128)} %get-tuple-element.22, f32[1,640,2560]{2,1,0:T(8,128)} %get-tuple-element.32, f32[1,640,2560]{2,1,0:T(8,128)} %get-tuple-element.33), kind=kOutput, calls=%fused_computation.62 | convolution fusion | flops 6311116800 | bytes 27852800 | tf_op jit(solution)/shard_map/hvcpl,cpn->hlvn/dot_general | solution.py:125
  515.7 5.0 copy.132
  520.7 9.9 %reshape.537 = f32[8,1,25600]{2,1,0:T(1,128)S(1)} reshape(f32[2560,2,2,20]{3,2,1,0:T(2,128)} %bitcast.92) | data formatting | bytes 1638400
  530.6 17.1 %all_to_all.69 = f32[8,1,25600]{2,1,0:T(1,128)S(1)} all-to-all(f32[8,1,25600]{2,1,0:T(1,128)S(1)} %reshape.537), channel_id=1, replica_groups=mesh['band'=4,'sector'=8] {'sector'}, dimensions={0} | all-to-all | bytes 1638400 | tf_op jit(solution)/shard_map/all_to_all | solution.py:131
  547.7 2.6 reduce.1
  550.3 10.9 %reshape.538 = f32[2560,2,2,20]{3,2,1,0:T(2,128)} reshape(f32[8,25600]{1,0:T(8,128)S(1)} %reduce.1) | data formatting | bytes 1638400
  561.1 5.0 copy.144
  566.2 1.5 copy.134
  (18 shorter events, 0.1 us)
Async XLA Ops:
  8.2 79.9 %collective-permute-start = (f32[2,160,2,96]{1,3,2,0:T(8,128)S(1)}, f32[2,160,2,96]{1,3,2,0:T(8,128)S(1)}, u32[]{:S(2)}, u32[]{:S(2)}) collective-permute-start(f32[2,160,2,96]{1,3,2,0:T(8,128)S(1)} %get-tuple-element.15), channel_id=1, source_target_pairs={{0,1},{1,2},{2,3},{3,4},{4,5},{5,6},{6,7},{7,0},{8,9},{9,10},{10,1... | collective-permute-start | bytes 737288 | tf_op jit(solution)/shard_map/ppermute | solution.py:17
  8.7 79.4 %collective-permute-start.1 = (f32[2,160,2,96]{1,3,2,0:T(8,128)S(1)}, f32[2,160,2,96]{1,3,2,0:T(8,128)S(1)}, u32[]{:S(2)}, u32[]{:S(2)}) collective-permute-start(f32[2,160,2,96]{1,3,2,0:T(8,128)S(1)} %get-tuple-element.16), channel_id=1, source_target_pairs={{1,0},{2,1},{3,2},{4,3},{5,4},{6,5},{7,6},{0,7},{9,8},{10,9},{11,1... | collective-permute-start | bytes 737288 | tf_op jit(solution)/shard_map/ppermute | solution.py:18
  11.6 28.4 %copy-start.1 = (s32[2,160,10]{1,0,2:T(2,128)S(1)}, s32[2,160,10]{1,0,2:T(2,128)}, u32[]{:S(2)}) copy-start(s32[2,160,10]{1,0,2:T(2,128)} %param.6) | copy-start | bytes 38404
  144.2 31.9 %all-to-all-start = ((f32[2,160,2,320]{3,2,0,1:T(2,128)}), f32[2,160,2,320]{3,2,0,1:T(2,128)S(1)}, u32[]{:S(2)}, u32[]{:S(2)}) async-start(f32[2,160,2,320]{3,2,0,1:T(2,128)} %copy.116), calls=%async_computation | async-start | bytes 1966080 | tf_op jit(solution)/shard_map/all_to_all | solution.py:108
  211.6 17.1 %all-to-all-start.1 = ((f32[8,1,25600]{2,1,0:T(1,128)}), f32[8,1,25600]{2,1,0:T(1,128)S(1)}, u32[]{:S(2)}, u32[]{:S(2)}) async-start(f32[8,1,25600]{2,1,0:T(1,128)} %reshape.535), calls=%async_computation.1 | async-start | bytes 1638400 | tf_op jit(solution)/shard_map/all_to_all | solution.py:116
  215.8 161.2 %all-reduce.2.cloned.1.call-start = ((), (), s32[]{:S(2)}) async-start(), calls=%async_computation.4 | async-start | bytes 3604480 | tf_op jit(solution)/shard_map/psum | solution.py:121
  250.4 42.8 %copy-start = (pred[80,1281]{1,0:T(8,128)(4,1)S(1)}, pred[80,1281]{1,0:T(8,128)(4,1)}, u32[]{:S(2)}) copy-start(pred[80,1281]{1,0:T(8,128)(4,1)} %get-tuple-element.26) | copy-start | bytes 307444
  297.6 2.7 copy-start.2
  461.4 33.8 %all-to-all-start.2 = ((f32[2,2,4,80,160]{3,2,1,0,4:T(4,128)}), f32[2,2,4,80,160]{3,2,1,0,4:T(4,128)S(1)}, u32[]{:S(2)}, u32[]{:S(2)}) async-start(f32[2,2,4,80,160]{3,2,1,0,4:T(4,128)} %copy.128), calls=%async_computation.2 | async-start | bytes 2621440 | tf_op jit(solution)/shard_map/all_to_all | solution.py:124
Sparse Core Ops, SparseCore 0:
  300.4 76.5 all-reduce.1
where the time goes:
time: 584 us; the launch traced here: 575 us
  matrix products  198 us (34%)
  other arithmetic  140 us (24%)
  local copies, waits for them, and re-layouts  130 us (22%)
  waiting for transfers between devices  59.6 us (10%)
  blocking collectives  17.1 us (3%)
  starting transfers between devices  15.9 us (3%)
  between operations  13.9 us (2%)
    unnamed x12, local copies, waits for them, and re-layouts  91.7 us
    dot_general x1, matrix products, synthesise(): return jnp.einsum('hvcpk,plk->hvcpl', stacked, legendre, precision=HIGHEST)  73.3 us
    psum x1, waiting for transfers between devices, local(): summed = lax.psum(partial_value, 'band')  48 us
    dot_general x1, matrix products, advect(): jnp.einsum('hlvtj,hltji->hlvti', window, interp_weight.astype(jnp.float32...  43.8 us
    dot_general x1, matrix products, analyse(): jnp.einsum('svcpl,plk->svcpk', stacked, legendre, precision=HIGHEST)  42.7 us
    mul x1, other arithmetic, inverse_table(): 2.0 * jnp.cos(upper_angle)  29.7 us
    cos x1, other arithmetic, forward_table(): jnp.cos(upper_angle)  28.4 us
    mul x1, other arithmetic, inverse_table(): -lower_scale * jnp.sin(lower_angle)  28.3 us
  transfers between devices with their start and end apart: 6, of which 2 were waited for; matrix products, arithmetic and copies ran while one was open for 29% of the time, Pallas kernels for 0%

commit v1 on v0

--- a/solution.py
+++ b/solution.py
@@ -118,7 +118,9 @@
     pair_index = lax.axis_index("sector") * pair_local + jnp.arange(pair_local, dtype=jnp.int32)
     leading, odd_rows, degree = pair_masks(pair_index, m_count, row_count)
     partial_value = analyse(wave, legendre, leading, odd_rows)
-    summed = lax.psum(partial_value, "band")
+    summed = partial_value
+    for hop in (1, 2):
+        summed = summed + lax.ppermute(summed, "band", [(dev, dev ^ hop) for dev in range(4)])
     spectrum = solve_modes(summed, damping, degree, m_count)
     synthesis = synthesise(spectrum, legendre, leading, odd_rows)
     returned = lax.all_to_all(synthesis, "sector", split_axis=4, concat_axis=3, tiled=True)

time: 584 us -> 614 us (1.051)
  waiting for transfers between devices: 59.6 us -> 94.6 us
  between operations: 13.9 us -> 0.55 us
  starting transfers between devices: 15.9 us -> 25.2 us
    ppermute x0 -> x2, waiting for transfers between devices: none -> 82.1 us  [local(): lax.ppermute(summed, 'band', [(dev, dev ^ hop) for dev in range(4)])]
    psum x1 -> x0, waiting for transfers between devices: 48 us -> none  [local(): summed = lax.psum(partial_value, 'band')]
    unnamed x12 -> x10, local copies, waits for them, and re-layouts: 91.7 us -> 91.8 us
  transfers between devices with their start and end apart: 6 -> 7, of which waited for: 2 -> 3; matrix products, arithmetic and copies ran while one was open for 29% -> 27% of each run, Pallas kernels for 0% -> 0%
where the time goes in v1:
time: 614 us; the launch traced here: 604 us
  matrix products  198 us (32%)
  other arithmetic  139 us (23%)
  local copies, waits for them, and re-layouts  130 us (21%)
  waiting for transfers between devices  94.6 us (15%)
  starting transfers between devices  25.2 us (4%)
  blocking collectives  17.1 us (3%)
    unnamed x10, local copies, waits for them, and re-layouts  91.8 us
    ppermute x2, waiting for transfers between devices, local(): lax.ppermute(summed, 'band', [(dev, dev ^ hop) for dev in range(4)])  82.1 us
    dot_general x1, matrix products, synthesise(): return jnp.einsum('hvcpk,plk->hvcpl', stacked, legendre, precision=HIGHEST)  73 us
    dot_general x1, matrix products, advect(): jnp.einsum('hlvtj,hltji->hlvti', window, interp_weight.astype(jnp.float32...  43.8 us
    dot_general x1, matrix products, analyse(): jnp.einsum('svcpl,plk->svcpk', stacked, legendre, precision=HIGHEST)  42.9 us
    mul x1, other arithmetic, inverse_table(): 2.0 * jnp.cos(upper_angle)  29.7 us
    cos x1, other arithmetic, forward_table(): jnp.cos(upper_angle)  28.3 us
    mul x1, other arithmetic, inverse_table(): -lower_scale * jnp.sin(lower_angle)  28.3 us
  transfers between devices with their start and end apart: 7, of which 3 were waited for; matrix products, arithmetic and copies ran while one was open for 27% of the time, Pallas kernels for 0%

profile of v1, /device:TPU:0, one launch (start us, length us, event | category | flops | bytes accessed | tf_op | source)
XLA Modules:
  0.0 604.3 jit_solution(10196253147172846542)
XLA Ops:
  0.0 1.6 copy.106
  1.6 0.1 fusion.71
  1.6 0.5 collective-permute-start
  2.2 2.9 collective-permute-start.1
  5.1 28.3 %fusion.32 = (f32[2560,1,640]{2,0,1:T(8,128)}, f32[2560,1,640]{2,0,1:T(8,128)}) fusion(s32[640]{0:T(1024)S(1)} %iota_subtract_fusion), kind=kLoop, calls=%fused_computation.40 | loop fusion | flops 16384000 | bytes 13109760 | tf_op jit(solution)/shard_map/cos | solution.py:33
  33.5 0.1 broadcast_compare_fusion.4
  33.6 47.9 %copy.114 = bf16[2,160,10,64,32]{3,4,2,1,0:T(8,128)(2,1)} copy(bf16[2,160,10,64,32]{1,4,3,2,0:T(8,128)(2,1)} %param.7) | data formatting | bytes 26214400 | tf_op args[2]
  81.6 0.1 pad_maximum_fusion.1
  81.7 1.0 fusion.70
  82.7 1.8 maximum_select_fusion
  84.5 3.6 copy.113
  88.1 43.8 %convolution_bitcast_fusion = f32[2,160,2,10,32]{4,2,3,1,0:T(2,128)S(1)} fusion(f32[2,160,2,10,64]{4,2,3,1,0:T(2,128)} %copy.113, bf16[2,160,10,64,32]{3,4,2,1,0:T(8,128)(2,1)} %copy.114), kind=kOutput, calls=%fused_computation.67 | convolution fusion | flops 157286400 | bytes 15564800 | tf_op jit(solution)/shard_map/hlvtj,hltji->hlvti/dot_general | solution.py:100
  131.9 3.4 copy.115
  135.3 2.4 copy.116
  137.6 3.8 all-to-all-start
  141.5 27.9 %sine_negate_fusion.1 = (f32[2560,1,640]{2,0,1:T(8,128)}, f32[2560,1,640]{2,0,1:T(8,128)}) fusion(), kind=kLoop, calls=%fused_computation.41 | loop fusion | flops 16384000 | bytes 13107200 | tf_op jit(solution)/shard_map/neg | solution.py:33
  169.4 0.3 copy.140
  169.7 0.3 reshape.528
  170.0 19.3 %fusion.54 = f32[2,2,4,640,20]{3,4,1,0,2:T(8,128)S(1)} fusion(f32[2,20,2,2560,1]{3,1,2,0,4:T(8,128)S(1)} %reshape.528, f32[2560,1,640]{2,0,1:T(8,128)} %get-tuple-element.25, f32[2560,1,640]{2,0,1:T(8,128)} %get-tuple-element.24, f32[2560,1,640]{2,0,1:T(8,128)} %get-tuple-element.30, f32[2560,1,640]{2,0,1:T(8,128)} %get-tuple-element.31), kind=kOutput, calls=%fused_computation.79 | convolution fusion | flops 6317670400 | bytes 27852800 | tf_op jit(solution)/shard_map/hlvn,ncp->hvcpl/dot_general | solution.py:113
  189.3 5.0 copy.120
  194.3 10.6 %reshape.535 = f32[8,1,25600]{2,1,0:T(1,128)} reshape(f32[640,4,2,2,20]{4,3,2,1,0:T(2,128)} %bitcast.90) | data formatting | bytes 1638400
  204.9 4.7 all-to-all-start.1
  209.7 0.4 fusion.61
  210.0 12.5 %all-to-all-done.1 = f32[8,1,25600]{2,1,0:T(1,128)S(1)} async-done(((f32[8,1,25600]{2,1,0:T(1,128)}), f32[8,1,25600]{2,1,0:T(1,128)S(1)}, u32[]{:S(2)}, u32[]{:S(2)}) %all-to-all-start.1) | async-done | bytes 819232 | tf_op jit(solution)/shard_map/all_to_all | solution.py:116
  222.5 0.5 broadcast.505
  223.0 2.6 reduce
  225.6 10.9 %reshape.536 = f32[640,4,2,2,20]{4,3,2,1,0:T(2,128)} reshape(f32[8,25600]{1,0:T(8,128)S(1)} %reduce) | data formatting | bytes 1638400
  236.5 5.8 copy.141
  242.3 0.2 slice_add_fusion
  242.5 0.2 copy.122
  242.7 0.4 copy.124
  243.1 0.2 copy.123
  243.3 0.4 copy.125
  243.7 0.3 fusion.84
  244.1 42.9 %fusion.44 = f32[2,2,4,80,1281]{4,2,1,0,3:T(4,128)} fusion(f32[80,160,1281]{2,1,0:T(8,128)} %param.8, f32[2,2,4,80,160]{4,2,1,0,3:T(4,128)S(1)} %fusion.84), kind=kOutput, calls=%fused_computation.61 | convolution fusion | flops 3148185600 | bytes 72965120 | tf_op jit(solution)/shard_map/svcpl,plk->svcpk/dot_general | solution.py:68
  286.9 4.5 fusion.48
  291.4 1.4 slice_select_fusion
  292.8 2.3 collective-permute-start.2
  295.1 0.2 fusion.63
  295.4 36.3 %collective-permute-done.2 = f32[2,2,80,1281]{3,1,0,2:T(2,128)S(1)} collective-permute-done((f32[2,2,80,1281]{3,1,0,2:T(2,128)S(1)}, f32[2,2,80,1281]{3,1,0,2:T(2,128)S(1)}, u32[]{:S(2)}, u32[]{:S(2)}) %collective-permute-start.2) | collective-permute-done | bytes 1639712 | tf_op jit(solution)/shard_map/ppermute | solution.py:123
  331.7 1.7 fusion.77
  333.4 2.8 collective-permute-start.3
  336.2 0.5 multiply_add_fusion
  336.7 28.3 %sine_multiply_fusion.1 = (f32[1,640,2560]{2,1,0:T(8,128)}, f32[1,640,2560]{2,1,0:T(8,128)}) fusion(f32[640]{0:T(1024)S(1)} %fusion.65, f32[640]{0:T(1024)S(1)} %fusion.64), kind=kLoop, calls=%fused_computation.51 | loop fusion | flops 18022400 | bytes 13112320 | tf_op jit(solution)/shard_map/mul | solution.py:48
  365.0 45.8 %collective-permute-done.3 = f32[2,2,80,1281]{3,1,0,2:T(2,128)S(1)} collective-permute-done((f32[2,2,80,1281]{3,1,0,2:T(2,128)S(1)}, f32[2,2,80,1281]{3,1,0,2:T(2,128)S(1)}, u32[]{:S(2)}, u32[]{:S(2)}) %collective-permute-start.3) | collective-permute-done | bytes 1639712 | tf_op jit(solution)/shard_map/ppermute | solution.py:123
  410.7 2.3 broadcast_select_fusion.1
  413.0 1.1 broadcast_select_fusion
  414.2 1.1 fusion.76
  415.3 1.7 maximum_bitcast_fusion.4
  417.0 2.4 negate_select_fusion
  419.4 73.0 %fusion.49 = f32[2,2,4,80,160]{4,2,1,0,3:T(4,128)S(1)} fusion(f32[80,160,1281]{2,1,0:T(8,128)} %param.8, f32[1,2,4,80,1281]{4,2,1,3,0:T(4,128)S(1)} %negate_select_fusion, f32[1,2,4,80,1281]{4,2,1,3,0:T(4,128)S(1)} %maximum_bitcast_fusion.4), kind=kOutput, calls=%fused_computation.78 | convolution fusion | flops 3149825280 | bytes 72965120 | tf_op jit(solution)/shard_map/hvcpk,plk->hvcpl/dot_general | solution.py:84
  492.4 1.7 copy.128
  494.1 8.0 %all-to-all-start.2 = ((f32[2,2,4,80,160]{3,2,1,0,4:T(4,128)}), f32[2,2,4,80,160]{3,2,1,0,4:T(4,128)S(1)}, u32[]{:S(2)}, u32[]{:S(2)}) async-start(f32[2,2,4,80,160]{3,2,1,0,4:T(4,128)} %copy.128), calls=%async_computation.2 | async-start | bytes 2621440 | tf_op jit(solution)/shard_map/all_to_all | solution.py:126
  502.1 29.7 %cosine_multiply_fusion = (f32[1,640,2560]{2,1,0:T(8,128)}, f32[1,640,2560]{2,1,0:T(8,128)}) fusion(s32[640]{0:T(1024)S(1)} %iota_subtract_fusion), kind=kLoop, calls=%fused_computation.47 | loop fusion | flops 18022400 | bytes 13109760 | tf_op jit(solution)/shard_map/mul | solution.py:49
  531.8 0.8 copy.143
  532.5 0.5 reshape.534
  533.0 19.2 %fusion.47 = f32[2,20,2,2560]{3,1,2,0:T(8,128)S(1)} fusion(f32[2,2,4,640,20]{3,4,2,1,0:T(8,128)S(1)} %reshape.534, f32[1,640,2560]{2,1,0:T(8,128)} %get-tuple-element.23, f32[1,640,2560]{2,1,0:T(8,128)} %get-tuple-element.22, f32[1,640,2560]{2,1,0:T(8,128)} %get-tuple-element.32, f32[1,640,2560]{2,1,0:T(8,128)} %get-tuple-element.33), kind=kOutput, calls=%fused_computation.62 | convolution fusion | flops 6311116800 | bytes 27852800 | tf_op jit(solution)/shard_map/hvcpl,cpn->hlvn/dot_general | solution.py:127
  552.3 4.9 copy.132
  557.2 9.9 %reshape.537 = f32[8,1,25600]{2,1,0:T(1,128)S(1)} reshape(f32[2560,2,2,20]{3,2,1,0:T(2,128)} %bitcast.92) | data formatting | bytes 1638400
  567.1 17.1 %all_to_all.69 = f32[8,1,25600]{2,1,0:T(1,128)S(1)} all-to-all(f32[8,1,25600]{2,1,0:T(1,128)S(1)} %reshape.537), channel_id=1, replica_groups=mesh['band'=4,'sector'=8] {'sector'}, dimensions={0} | all-to-all | bytes 1638400 | tf_op jit(solution)/shard_map/all_to_all | solution.py:133
  584.2 2.6 reduce.1
  586.8 10.9 %reshape.538 = f32[2560,2,2,20]{3,2,1,0:T(2,128)} reshape(f32[8,25600]{1,0:T(8,128)S(1)} %reduce.1) | data formatting | bytes 1638400
  597.7 5.0 copy.144
  602.7 1.5 copy.134
  (18 shorter events, 0.1 us)
Async XLA Ops:
  1.6 79.9 %collective-permute-start = (f32[2,160,2,96]{1,3,2,0:T(8,128)S(1)}, f32[2,160,2,96]{1,3,2,0:T(8,128)S(1)}, u32[]{:S(2)}, u32[]{:S(2)}) collective-permute-start(f32[2,160,2,96]{1,3,2,0:T(8,128)S(1)} %get-tuple-element.15), channel_id=1, source_target_pairs={{0,1},{1,2},{2,3},{3,4},{4,5},{5,6},{6,7},{7,0},{8,9},{9,10},{10,1... | collective-permute-start | bytes 737288 | tf_op jit(solution)/shard_map/ppermute | solution.py:17
  2.2 79.4 %collective-permute-start.1 = (f32[2,160,2,96]{1,3,2,0:T(8,128)S(1)}, f32[2,160,2,96]{1,3,2,0:T(8,128)S(1)}, u32[]{:S(2)}, u32[]{:S(2)}) collective-permute-start(f32[2,160,2,96]{1,3,2,0:T(8,128)S(1)} %get-tuple-element.16), channel_id=1, source_target_pairs={{1,0},{2,1},{3,2},{4,3},{5,4},{6,5},{7,6},{0,7},{9,8},{10,9},{11,1... | collective-permute-start | bytes 737288 | tf_op jit(solution)/shard_map/ppermute | solution.py:18
  5.1 28.4 %copy-start = (s32[2,160,10]{1,0,2:T(2,128)S(1)}, s32[2,160,10]{1,0,2:T(2,128)}, u32[]{:S(2)}) copy-start(s32[2,160,10]{1,0,2:T(2,128)} %param.6) | copy-start | bytes 38404
  137.6 31.8 %all-to-all-start = ((f32[2,160,2,320]{3,2,0,1:T(2,128)}), f32[2,160,2,320]{3,2,0,1:T(2,128)S(1)}, u32[]{:S(2)}, u32[]{:S(2)}) async-start(f32[2,160,2,320]{3,2,0,1:T(2,128)} %copy.116), calls=%async_computation | async-start | bytes 1966080 | tf_op jit(solution)/shard_map/all_to_all | solution.py:108
  204.9 17.6 %all-to-all-start.1 = ((f32[8,1,25600]{2,1,0:T(1,128)}), f32[8,1,25600]{2,1,0:T(1,128)S(1)}, u32[]{:S(2)}, u32[]{:S(2)}) async-start(f32[8,1,25600]{2,1,0:T(1,128)} %reshape.535), calls=%async_computation.1 | async-start | bytes 1638400 | tf_op jit(solution)/shard_map/all_to_all | solution.py:116
  292.8 38.9 %collective-permute-start.2 = (f32[2,2,80,1281]{3,1,0,2:T(2,128)S(1)}, f32[2,2,80,1281]{3,1,0,2:T(2,128)S(1)}, u32[]{:S(2)}, u32[]{:S(2)}) collective-permute-start(f32[2,2,80,1281]{3,1,0,2:T(2,128)S(1)} %slice_select_fusion), channel_id=1, source_target_pairs={{0,8},{8,0},{16,24},{24,16},{1,9},{9,1},{17,25},{25,17},{2,10},{10... | collective-permute-start | bytes 4919048 | tf_op jit(solution)/shard_map/ppermute | solution.py:123
  295.4 40.9 %copy-start.1 = (f32[2]{0:T(128)S(1)}, f32[2]{0:T(128)}, u32[]{:S(2)}) copy-start(f32[2]{0:T(128)} %param.9) | copy-start | bytes 28
  333.4 77.3 %collective-permute-start.3 = (f32[2,2,80,1281]{3,1,0,2:T(2,128)S(1)}, f32[2,2,80,1281]{3,1,0,2:T(2,128)S(1)}, u32[]{:S(2)}, u32[]{:S(2)}) collective-permute-start(f32[2,2,80,1281]{3,1,0,2:T(2,128)S(1)} %fusion.77), channel_id=1, source_target_pairs={{0,16},{8,24},{16,0},{24,8},{1,17},{9,25},{17,1},{25,9},{2,18},{10... | collective-permute-start | bytes 4919048 | tf_op jit(solution)/shard_map/ppermute | solution.py:123
  494.1 37.7 %all-to-all-start.2 = ((f32[2,2,4,80,160]{3,2,1,0,4:T(4,128)}), f32[2,2,4,80,160]{3,2,1,0,4:T(4,128)S(1)}, u32[]{:S(2)}, u32[]{:S(2)}) async-start(f32[2,2,4,80,160]{3,2,1,0,4:T(4,128)} %copy.128), calls=%async_computation.2 | async-start | bytes 2621440 | tf_op jit(solution)/shard_map/all_to_all | solution.py:126
